TPU v7x, 32 devices: a whole 2x2x4 slice. The times are simulated.
32 devices in a mesh: sa: 8 (over z, x), ka: 2 (over y), vert: 2 (over core).
Axes of the slice: x: 2, y: 2, z: 4, core: 2. Of those that a mesh axis runs over, the one named last changes fastest.
Arguments:
- queries: bfloat16 [1024, 16, 128], P('sa', None, 'ka'), may hold values from -6 to 6
- key_rows: bfloat16 [1024, 16, 128], P('sa', None, 'ka'), may hold values from -6 to 6
- values: bfloat16 [1024, 16, 256], P('sa', None, 'vert'), may hold values from -6 to 6
- log_decays: bfloat16 [1024, 16, 128], P('sa', None, 'ka'), may hold values from -2 to 0
- output_grad: bfloat16 [1024, 16, 256], P('sa', None, 'vert'), may hold values from -0.1875 to 0.1875
Outputs:
- query_grad: float32 [1024, 16, 128], P('sa', 'vert', 'ka')
- key_grad: float32 [1024, 16, 128], P('sa', 'vert', 'ka')
- value_grad: float32 [1024, 16, 256], P('sa', 'ka', 'vert')
- decay_grad: float32 [1024, 16, 128], P('sa', 'vert', 'ka')
All inputs are finite; a program needn't handle non-finite values.
Results may differ from a plain program's by a relative error of at most 0.0003.
Values may be sent and summed in bfloat16 or wider, within the bound.
A program may use at most 192 MiB of HBM per device.

v0:
```python
import jax
import jax.numpy as jnp
from jax import lax
from jax.sharding import PartitionSpec as P

DK = 128
TILE_LEN = 64


largest_entry = lax.Precision.HIGHEST


def entering(value, axis, join, neutral, backward):
    count, mine = (lax.axis_size(axis), lax.axis_index(axis))
    pieces = jax.tree.map(lambda part: lax.all_gather(part, axis), value)
    if backward:
        pieces = jax.tree.map(lambda part: part[::-1], pieces)
        mine = count - 1 - mine
    total = jax.tree.map(
        lambda part, zero: jnp.full_like(part, 0) + jnp.asarray(zero, part.dtype), value, neutral
    )

    def hop(position, total):
        longer = join(total, jax.tree.map(lambda part: part[position], pieces))
        return jax.tree.map(lambda new, old: jnp.where(position < mine, new, old), longer, total)

    return lax.fori_loop(0, count - 1, hop, total)


def to_blocks(tensor, length):
    row_count, head_count, channels = tensor.shape
    return (
        tensor.astype(jnp.float32)
        .reshape(row_count // length, length, head_count, channels)
        .transpose(0, 2, 1, 3)
    )


def from_blocks(tensor):
    tile_count, head_count, length, channels = tensor.shape
    return tensor.transpose(0, 2, 1, 3).reshape(tile_count * length, head_count, channels)


def causal(length):
    row_ids = lax.broadcasted_iota(jnp.int32, (length, length), 0)
    col_ids = lax.broadcasted_iota(jnp.int32, (length, length), 1)
    return row_ids >= col_ids


def compose(earlier, later):
    return (earlier[0] * later[0], later[0][..., None] * earlier[1] + later[1])


def advance(carried_over, step_terms):
    return (step_terms[0][..., None] * carried_over + step_terms[1], carried_over)


def backward_states(scaled, cumulative, cotangent):
    tile_total = cumulative[:, :, -1, :]
    amplified_query = scaled * jnp.exp(cumulative)
    terms = jnp.einsum("nhik,nhiv->nhkv", amplified_query, cotangent, precision=largest_entry)
    leading, ends = lax.scan(
        advance, jnp.zeros_like(terms[0]), (jnp.exp(tile_total), terms), reverse=True
    )
    after = jnp.sum(tile_total, 0) - jnp.cumsum(tile_total, 0)
    return (amplified_query, ends, leading, after)


def value_terms(amplified_query, shrunk_key, attenuated_key, cotangent, ends, lower_mask):
    weights = jnp.where(
        lower_mask,
        jnp.einsum("nhik,nhjk->nhij", amplified_query, shrunk_key, precision=largest_entry),
        0.0,
    )
    local_part = jnp.einsum("nhij,nhiv->nhjv", weights, cotangent, precision=largest_entry)
    return local_part + jnp.einsum("nhjk,nhkv->nhjv", attenuated_key, ends, precision=largest_entry)


def gradient_core(queries, key_rows, values, log_decays, output_grad):
    factor = DK ** (-0.5)
    scaled = to_blocks(queries, TILE_LEN) * factor
    keyed = to_blocks(key_rows, TILE_LEN)
    valued = to_blocks(values, TILE_LEN)
    cotangent = to_blocks(output_grad, TILE_LEN)
    cumulative = jnp.cumsum(to_blocks(log_decays, TILE_LEN), axis=2)
    tile_total = cumulative[:, :, -1, :]
    growth = jnp.exp(cumulative)
    shrink = jnp.exp(-cumulative)
    until_finish = jnp.exp(tile_total[:, :, None, :] - cumulative)
    shrunk_key = keyed * shrink
    attenuated_key = keyed * until_finish
    forward_terms = jnp.einsum("nhjk,nhjv->nhkv", attenuated_key, valued, precision=largest_entry)
    shard_state, starts = lax.scan(
        advance, jnp.zeros_like(forward_terms[0]), (jnp.exp(tile_total), forward_terms)
    )
    amplified_query, ends, shard_back, after = backward_states(scaled, cumulative, cotangent)
    shard_decay = jnp.exp(jnp.sum(tile_total, 0))
    identity = (jnp.ones_like(shard_decay), jnp.zeros_like(shard_state))
    incoming = entering((shard_decay, shard_state), "sa", compose, identity, False)[1]
    outgoing = entering((shard_decay, shard_back), "sa", compose, identity, True)[1]
    before = jnp.cumsum(tile_total, 0) - tile_total
    starts = starts + jnp.exp(before)[..., None] * incoming[None]
    ends = ends + jnp.exp(after)[..., None] * outgoing[None]
    lower_mask = causal(TILE_LEN)
    scores = jnp.where(
        lower_mask, jnp.einsum("nhiv,nhjv->nhij", cotangent, valued, precision=largest_entry), 0.0
    )
    query_local = jnp.einsum("nhij,nhjk->nhik", scores, shrunk_key, precision=largest_entry)
    query_carried = jnp.einsum("nhiv,nhkv->nhik", cotangent, starts, precision=largest_entry)
    query_part = growth * (query_local + query_carried) * factor
    key_local = shrink * jnp.einsum(
        "nhij,nhik->nhjk", scores, amplified_query, precision=largest_entry
    )
    key_part = key_local + until_finish * jnp.einsum(
        "nhjv,nhkv->nhjk", valued, ends, precision=largest_entry
    )
    pieces = (amplified_query, shrunk_key, attenuated_key, cotangent, ends, lower_mask)
    return (query_part, key_part, pieces, outgoing)


def later_sums(position_grad):
    shard_rows = position_grad.shape[0]
    head_span = position_grad.shape[1]
    tile_rows = position_grad.reshape(
        shard_rows // TILE_LEN, TILE_LEN, head_span, position_grad.shape[2]
    )
    upper = causal(TILE_LEN).T.astype(jnp.float32)
    within = jnp.einsum("ij,njhk->nihk", upper, tile_rows, precision=largest_entry)
    tile_sums = jnp.sum(tile_rows, 1)
    later = jnp.sum(tile_sums, 0) - jnp.cumsum(tile_sums, 0)
    shard_sum = jnp.sum(tile_sums, 0)
    gathered = lax.all_gather(shard_sum[None], "sa", axis=0, tiled=True)
    owners = lax.broadcasted_iota(jnp.int32, (gathered.shape[0],), 0)
    weights = (owners > lax.axis_index("sa")).astype(jnp.float32)
    beyond = jnp.einsum("a,ahk->hk", weights, gathered, precision=largest_entry)
    return (within + later[:, None] + beyond[None, None]).reshape(position_grad.shape)


def shards(queries, key_rows, values, log_decays, output_grad):
    query_part, key_part, pieces, outgoing = gradient_core(
        queries, key_rows, values, log_decays, output_grad
    )
    amplified_query, shrunk_key, attenuated_key, cotangent, ends, lower_mask = pieces
    query_grad, key_grad = (
        lax.psum_scatter(from_blocks(query_part), "vert", scatter_dimension=1, tiled=True),
        lax.psum_scatter(from_blocks(key_part), "vert", scatter_dimension=1, tiled=True),
    )
    value_part = value_terms(
        amplified_query, shrunk_key, attenuated_key, cotangent, ends, lower_mask
    )
    value_grad = lax.psum_scatter(from_blocks(value_part), "ka", scatter_dimension=1, tiled=True)
    head_half = queries.shape[1] // lax.axis_size("vert")
    first_head = lax.axis_index("vert") * head_half
    own_query = lax.dynamic_slice_in_dim(queries, first_head, head_half, 1).astype(jnp.float32)
    own_key = lax.dynamic_slice_in_dim(key_rows, first_head, head_half, 1).astype(jnp.float32)
    position_grad = own_query * query_grad - own_key * key_grad
    decay_grad = later_sums(position_grad)
    return (query_grad, key_grad, value_grad, decay_grad)


def solution(mesh):
    return jax.shard_map(
        shards,
        mesh=mesh,
        in_specs=(
            P("sa", None, "ka"),
            P("sa", None, "ka"),
            P("sa", None, "vert"),
            P("sa", None, "ka"),
            P("sa", None, "vert"),
        ),
        out_specs=(
            P("sa", "vert", "ka"),
            P("sa", "vert", "ka"),
            P("sa", "ka", "vert"),
            P("sa", "vert", "ka"),
        ),
        check_vma=False,
    )
```

profile of v0, /device:TPU:0, one launch (start us, length us, event | category | flops | bytes accessed | tf_op | source)
XLA Modules:
  0.0 257.4 jit_solution(14008535512210258950)
XLA Ops:
  7.2 1.4 copy.70
  8.7 13.2 %fusion.49 = f32[2,16,64,64]{3,1,2,0:T(8,128)S(1)} fusion(f32[2,16,64,64]{3,1,2,0:T(8,128)S(1)} %bitcast.150), kind=kOutput, calls=%fused_computation.81 | output fusion | flops 8257536 | bytes 1048576 | tf_op jit(solution)/shard_map/jit(cumsum)/reduce_window_sum | solution.py:85
  21.9 1.0 convert_multiply_fusion
  22.9 1.6 mul.166
  24.5 1.5 copy.51
  26.0 2.3 fusion.15
  28.3 1.1 broadcast.34.clone.1
  29.4 4.4 %while.60 = (s32[]{:T(128)}, f32[16,64,128]{2,1,0:T(8,128)S(1)}, f32[2,16,64,128]{3,2,1,0:T(8,128)}, f32[2,16,64]{2,1,0:T(8,128)S(1)}, f32[2,16,64,128]{3,2,1,0:T(8,128)}, /*index=5*/s32[]{:T(128)}, s32[]{:T(128)}) while((s32[]{:T(128)}, f32[16,64,128]{2,1,0:T(8,128)S(1)}, f32[2,16,64,128]{3,2,1,0:T(8,128)}, ...), condition=%wide.region_9.10_spmd.clone, body=%wide.region_8.9_spmd.clone.sunk | while | flops 524292 | bytes 2633840 | solution.py:62
  29.4 0.9 bitcast_dynamic-update-slice_fusion.5
  30.2 1.3 bitcast_add_fusion.7
  31.6 0.8 bitcast_dynamic-update-slice_fusion.5
  32.4 1.3 bitcast_add_fusion.7
  33.8 0.8 copy-done
  34.7 1.6 reshape.88
  36.3 1.5 copy.45
  37.8 2.3 fusion.17
  40.0 1.1 broadcast.34.clone
  41.1 4.4 %while.58 = (s32[]{:T(128)}, f32[16,64,128]{2,1,0:T(8,128)S(1)}, f32[2,16,64,128]{3,2,1,0:T(8,128)}, f32[2,16,64]{2,1,0:T(8,128)S(1)}, f32[2,16,64,128]{3,2,1,0:T(8,128)}, /*index=5*/s32[]{:T(128)}, s32[]{:T(128)}) while((s32[]{:T(128)}, f32[16,64,128]{2,1,0:T(8,128)S(1)}, f32[2,16,64,128]{3,2,1,0:T(8,128)}, ...), condition=%wide.region_2.3_spmd.clone, body=%wide.region_1.2_spmd.clone.sunk | while | flops 524291 | bytes 2634336 | solution.py:93
  41.1 0.9 bitcast_dynamic-update-slice_fusion.4
  42.0 1.3 bitcast_add_fusion.6
  43.4 0.9 bitcast_dynamic-update-slice_fusion.4
  44.2 1.4 bitcast_add_fusion.6
  45.6 0.8 copy-done.1
  46.5 33.1 %all-gather = f32[128,64]{1,0:T(8,128)S(1)} all-gather(f32[16,64]{1,0:T(8,128)S(1)} %exp.57), channel_id=2, replica_groups=mesh['sa'=8,'ka'=2,'vert'=2] {'sa'}, dimensions={0}, use_global_device_ids=true | all-gather | bytes 36864 | tf_op jit(solution)/shard_map/all_gather | solution.py:15
  80.3 2.6 %convolution_select_fusion = f32[2,16,64,64]{3,2,1,0:T(8,128)} fusion(pred[64,64]{1,0:T(8,128)(4,1)S(1)} %iota_compare_fusion, bf16[2,64,16,128]{3,2,1,0:T(8,128)(2,1)} %bitcast.147, bf16[2,64,16,128]{3,2,1,0:T(8,128)(2,1)} %bitcast.143), kind=kOutput, calls=%fused_computation.12 | convolution fusion | flops 33685504 | bytes 1576960 | tf_op jit(solution)/shard_map/nhiv,nhjv->nhij/dot_general | solution.py:106
  82.9 27.9 %all-gather.9.cloned.1.call-done = f32[128,64,128]{2,1,0:T(8,128)} async-done(((f32[16,64,128]{2,1,0:T(8,128)}), f32[128,64,128]{2,1,0:T(8,128)}) %all-gather.9.cloned.1.call-update) | async-done | bytes 4194320 | tf_op jit(solution)/shard_map/all_gather | solution.py:15
  110.8 4.7 %rev.7 = f32[8,16,64,128]{3,2,1,0:T(8,128)} reverse(f32[8,16,64,128]{3,2,1,0:T(8,128)} %bitcast.151), dimensions={0} | reverse | bytes 8388608 | tf_op jit(solution)/shard_map/rev | solution.py:17
  115.5 14.8 %while.61 = (s32[]{:T(128)}, f32[16,64,128]{2,1,0:T(8,128)S(1)}, s32[]{:T(128)}, f32[8,16,64]{2,1,0:T(8,128)}, f32[8,16,64,128]{3,2,1,0:T(8,128)}, /*index=5*/s32[]{:T(128)}, s32[]{:T(128)}) while((s32[]{:T(128)}, f32[16,64,128]{2,1,0:T(8,128)S(1)}, s32[]{:T(128)}, f32[8,16,64]{2,1,0:T(8,128)}, f32[8,16,64,128]{3,2,1,0:T(8,128)}, ...), condition=%wide.region_11.12_spmd.clone, body=%wide.region_10.11_spmd.clone.sunk | while | flops 524292 | bytes 1585257 | solution.py:27
  116.2 1.4 fusion.57
  117.6 0.7 dynamic-slice_bitcast_fusion.11
  118.3 1.4 fusion.57
  119.7 0.7 dynamic-slice_bitcast_fusion.11
  120.5 1.4 fusion.57
  121.9 0.7 dynamic-slice_bitcast_fusion.11
  122.6 1.4 fusion.57
  124.7 1.4 fusion.57
  126.1 0.7 dynamic-slice_bitcast_fusion.11
  126.8 1.4 fusion.57
  128.9 1.4 fusion.57
  130.3 2.9 %fusion.8 = f32[2,64,16,64]{3,1,2,0:T(8,128)S(1)} fusion(f32[2,16,64,128]{3,2,1,0:T(8,128)} %get-tuple-element.327, f32[2,16,64,64]{3,1,2,0:T(8,128)S(1)} %fusion.49, f32[16,64,128]{2,1,0:T(8,128)S(1)} %get-tuple-element.329, f32[2,16,64]{2,1,0:T(8,128)S(1)} %get-tuple-element.448, f32[2,16,64]{2,1,0:T(8,128)S(1)} %get-tuple-element.447, ...), kind=kOutput, calls=%fused_computation.24 | convolution fusion | flops 202113024 | bytes 3162112 | tf_op jit(solution)/shard_map/nhjv,nhkv->nhjk/dot_general | solution.py:114
  133.2 3.4 %fusion.4 = f32[2,64,16,64]{3,1,2,0:T(8,128)} fusion(f32[2,64,16,64]{3,1,2,0:T(8,128)S(1)} %fusion.8, f32[2,16,64,64]{3,2,1,0:T(8,128)S(1)} %copy-done.4, f32[2,16,64,64]{3,1,2,0:T(8,128)S(1)} %fusion.49, f32[2,64,16,64]{3,1,2,0:T(8,128)S(1)} %copy-done.3), kind=kOutput, calls=%fused_computation.17 | convolution fusion | flops 101187584 | bytes 2621440 | tf_op jit(solution)/shard_map/nhij,nhik->nhjk/dot_general | solution.py:111
  136.6 2.3 copy.55
  138.9 2.6 %reshape.83 = f32[128,16,64]{0,2,1:T(8,128)} reshape(f32[2,64,16,64]{1,0,3,2:T(2,128)} %copy.55) | data formatting | bytes 1048576 | tf_op jit(solution)/shard_map/reshape | solution.py:41
  141.8 43.1 %all-gather.7.cloned.1.call-done = f32[128,64,128]{2,1,0:T(8,128)} async-done(((f32[16,64,128]{2,1,0:T(8,128)}), f32[128,64,128]{2,1,0:T(8,128)}) %all-gather.7.cloned.1.call-update) | async-done | bytes 4194320 | tf_op jit(solution)/shard_map/all_gather | solution.py:15
  184.9 10.0 %while.59 = (s32[]{:T(128)}, f32[16,64,128]{2,1,0:T(8,128)S(1)}, s32[]{:T(128)}, f32[8,16,64]{2,1,0:T(8,128)S(1)}, f32[8,16,64,128]{3,2,1,0:T(8,128)}, /*index=5*/s32[]{:T(128)}, s32[]{:T(128)}) while((s32[]{:T(128)}, f32[16,64,128]{2,1,0:T(8,128)S(1)}, s32[]{:T(128)}, f32[8,16,64]{2,1,0:T(8,128)S(1)}, ...), condition=%wide.region_6.7_spmd.clone, body=%wide.region_5.6_spmd.clone.sunk | while | flops 524292 | bytes 1585257 | solution.py:27
  184.9 1.4 fusion.56
  186.3 1.4 fusion.56
  187.8 1.4 fusion.56
  189.2 1.4 fusion.56
  190.6 1.4 fusion.56
  192.0 1.4 fusion.56
  193.5 1.4 fusion.56
  194.9 2.5 convolution_bitcast_fusion.2
  197.4 4.1 %fusion.7 = f32[2,64,16,64]{3,1,2,0:T(8,128)} fusion(f32[2,64,16,64]{3,1,2,0:T(8,128)S(1)} %convolution_bitcast_fusion.2, f32[2,16,64,64]{3,2,1,0:T(8,128)} %convolution_select_fusion, f32[2,64,16,64]{3,1,2,0:T(8,128)S(1)} %copy.45, f32[2,16,64,64]{3,1,2,0:T(8,128)S(1)} %fusion.49), kind=kOutput, calls=%fused_computation.21 | convolution fusion | flops 101318656 | bytes 2621440 | tf_op jit(solution)/shard_map/nhij,nhjk->nhik/dot_general | solution.py:108
  201.4 2.3 copy.50
  203.7 2.7 %reshape.82 = f32[128,16,64]{0,2,1:T(8,128)} reshape(f32[2,64,16,64]{1,0,3,2:T(2,128)} %copy.50) | data formatting | bytes 1048576 | tf_op jit(solution)/shard_map/reshape | solution.py:41
  206.5 3.7 %convolution_select_fusion.1 = f32[2,16,64,64]{3,2,1,0:T(8,128)S(1)} fusion(f32[2,64,16,64]{3,1,2,0:T(8,128)S(1)} %copy.45, f32[2,16,64,64]{3,1,2,0:T(8,128)S(1)} %fusion.49, f32[2,64,16,64]{3,1,2,0:T(8,128)} %copy-done.2, pred[64,64]{1,0:T(8,128)(4,1)S(1)} %iota_compare_fusion), kind=kOutput, calls=%fused_computation.22 | convolution fusion | flops 101187584 | bytes 2101248 | tf_op jit(solution)/shard_map/nhik,nhjk->nhij/dot_general | solution.py:72
  210.3 1.0 fusion.20
  211.3 1.6 fusion.2
  212.9 1.6 copy.57
  214.5 1.2 fusion.48
  216.7 1.4 reduce_window_sum.36
  218.3 30.6 %all-gather.3 = f32[64,64]{1,0:T(8,128)S(1)} all-gather(f32[8,64]{1,0:T(8,128)S(1)} %get-tuple-element.442), channel_id=5, replica_groups=mesh['sa'=8,'ka'=2,'vert'=2] {'sa'}, dimensions={0}, use_global_device_ids=true | all-gather | bytes 18432 | tf_op jit(solution)/shard_map/all_gather | solution.py:132
  249.9 1.0 reshape.86
  (63 shorter events, 5.6 us)
Async XLA Ops:
  7.2 18.8 %copy-start.6 = (bf16[128,16,128]{2,1,0:T(8,128)(2,1)S(1)}, bf16[128,16,128]{2,1,0:T(8,128)(2,1)}, u32[]{:S(2)}) copy-start(bf16[128,16,128]{2,1,0:T(8,128)(2,1)} %param.17) | copy-start | bytes 1572868
  7.2 103.6 %all-gather.9.cloned.1.call-start = ((), (), s32[]{:S(2)}) async-start(), calls=%async_computation.7 | async-start | bytes 4718592 | tf_op jit(solution)/shard_map/all_gather | solution.py:15
  26.0 3.4 %copy-start.2 = (f32[2,64,16,64]{3,1,2,0:T(8,128)}, f32[2,64,16,64]{3,1,2,0:T(8,128)S(1)}, u32[]{:S(2)}) copy-start(f32[2,64,16,64]{3,1,2,0:T(8,128)S(1)} %copy.51) | copy-start | bytes 1572868
  29.4 5.3 %copy-start.10 = (bf16[128,16,64]{0,2,1:T(8,128)(2,1)S(1)}, bf16[128,16,64]{0,2,1:T(8,128)(2,1)}, u32[]{:S(2)}) copy-start(bf16[128,16,64]{0,2,1:T(8,128)(2,1)} %param.14) | copy-start | bytes 786436
  33.8 0.8 copy-start
  33.8 4.0 %copy-start.8 = (bf16[128,16,128]{2,1,0:T(8,128)(2,1)S(1)}, bf16[128,16,128]{2,1,0:T(8,128)(2,1)}, u32[]{:S(2)}) copy-start(bf16[128,16,128]{2,1,0:T(8,128)(2,1)} %param.15) | copy-start | bytes 1572868
  34.6 150.3 %all-gather.7.cloned.1.call-start = ((), (), s32[]{:S(2)}) async-start(), calls=%async_computation.6 | async-start | bytes 4718592 | tf_op jit(solution)/shard_map/all_gather | solution.py:15
  45.6 0.8 copy-start.1
  46.4 168.1 %reduce-scatter.6.cloned.1.call-start = ((), (), s32[]{:S(2)}) async-start(), calls=%async_computation.4 | async-start | bytes 786432 | tf_op jit(solution)/shard_map/reduce_scatter | solution.py:146
  130.3 2.9 %copy-start.3 = (f32[2,64,16,64]{3,1,2,0:T(8,128)S(1)}, f32[2,64,16,64]{3,1,2,0:T(8,128)}, u32[]{:S(2)}) copy-start(f32[2,64,16,64]{3,1,2,0:T(8,128)} %copy-done.2) | copy-start | bytes 1572868
  130.3 2.9 %copy-start.4 = (f32[2,16,64,64]{3,2,1,0:T(8,128)S(1)}, f32[2,16,64,64]{3,2,1,0:T(8,128)}, u32[]{:S(2)}) copy-start(f32[2,16,64,64]{3,2,1,0:T(8,128)} %convolution_select_fusion) | copy-start | bytes 1572868
  141.5 73.0 %reduce-scatter.4.cloned.1.call-start = ((), (), s32[]{:S(2)}) async-start(), calls=%async_computation.3 | async-start | bytes 786432 | tf_op jit(solution)/shard_map/reduce_scatter | solution.py:145
  203.7 6.5 %copy-start.7 = (bf16[128,16,128]{2,1,0:T(8,128)(2,1)S(1)}, bf16[128,16,128]{2,1,0:T(8,128)(2,1)}, u32[]{:S(2)}) copy-start(bf16[128,16,128]{2,1,0:T(8,128)(2,1)} %param.17) | copy-start | bytes 1572868
  206.4 44.5 %reduce-scatter.8.cloned.1.call-start = ((), (), s32[]{:S(2)}) async-start(), calls=%async_computation.5 | async-start | bytes 1572864 | tf_op jit(solution)/shard_map/reduce_scatter | solution.py:151
  206.5 4.8 %copy-start.5 = (f32[2,16,64,128]{3,2,1,0:T(8,128)S(1)}, f32[2,16,64,128]{3,2,1,0:T(8,128)}, u32[]{:S(2)}) copy-start(f32[2,16,64,128]{3,2,1,0:T(8,128)} %get-tuple-element.327) | copy-start | bytes 3145732
  211.3 3.3 %copy-start.9 = (bf16[128,16,64]{0,2,1:T(8,128)(2,1)S(1)}, bf16[128,16,64]{0,2,1:T(8,128)(2,1)}, u32[]{:S(2)}) copy-start(bf16[128,16,64]{0,2,1:T(8,128)(2,1)} %param.13) | copy-start | bytes 786436
Sparse Core Ops, SparseCore 0:
  34.7 75.9 all-gather.8
  113.5 71.4 all-gather.6
  187.7 6.4 reduce-scatter.5
  206.6 6.5 reduce-scatter.3
  215.8 21.4 reduce-scatter.7
where the time goes:
time: 259 us; the launch traced here: 257 us
  waiting for transfers between devices  71.2 us (27%)
  blocking collectives  63.7 us (25%)
  other arithmetic  45.7 us (18%)
  local copies, waits for them, and re-layouts  35 us (14%)
  matrix products  26.8 us (10%)
  between operations  14.1 us (5%)
    all_gather x2, waiting for transfers between devices, entering(): pieces = jax.tree.map(lambda part: lax.all_gather(part, axis), value)  71 us
    all_gather x1, blocking collectives, entering(): pieces = jax.tree.map(lambda part: lax.all_gather(part, axis), value)  33.1 us
    all_gather x1, blocking collectives, later_sums(): gathered = lax.all_gather(shard_sum[None], 'sa', axis=0, tiled=True)  30.6 us
    select_n x14, other arithmetic, hop(): jnp.where(position < mine, new, old)  19.4 us
    another operation x1, other arithmetic, gradient_core(): cumulative = jnp.cumsum(to_blocks(log_decays, TILE_LEN), axis=2)  13.2 us
    rev x2, local copies, waits for them, and re-layouts, entering(): pieces = jax.tree.map(lambda part: part[::-1], pieces)  5.38 us
    add x4, other arithmetic, advance(): step_terms[0][..., None] * carried_over + step_terms[1]  5.34 us
    reshape x2, local copies, waits for them, and re-layouts, from_blocks(): tensor.transpose(0, 2, 1, 3)  5.32 us
  transfers between devices with their start and end apart: 5, of which 2 were waited for; matrix products, arithmetic and copies ran while one was open for 31% of the time, Pallas kernels for 0%

commit v1 on v0

v1 whole, which is shorter than its diff:
```python
import functools

import jax
import jax.numpy as jnp
from jax import lax
from jax.experimental import pallas as pl
from jax.experimental.pallas import tpu as pltpu
from jax.sharding import PartitionSpec as P

F32 = jnp.float32
BF16 = jnp.bfloat16
MESH = pl.DeviceIdType.MESH
LAG = 2

NN = (((1,), (0,)), ((), ()))
NT = (((1,), (1,)), ((), ()))
TN = (((0,), (0,)), ((), ()))


def mm(a, b, dims):
    return lax.dot_general(a, b, dims, preferred_element_type=F32)


def split(a):
    high = a.astype(BF16)
    return high, (a - high.astype(F32)).astype(BF16)


def kernel(
    n,
    pairs,
    factor,
    q_ref,
    k_ref,
    v_ref,
    g_ref,
    o_ref,
    dq_ref,
    dk_ref,
    dv_ref,
    dg_ref,
    qs,
    ks,
    vs,
    gs,
    os,
    grow,
    shrink,
    ends,
    decay,
    decay_in,
    own,
    peer,
    f_in,
    b_in,
    f_out,
    b_out,
    entry,
    leave,
    qk,
    qk_in,
    vg,
    vg_in,
    x_send,
    x_recv,
    f_send,
    f_recv,
    b_send,
    b_recv,
    q_send,
    q_recv,
    v_send,
    v_recv,
    d_send,
    d_recv,
):
    rows, heads, kc = q_ref.shape
    vc = v_ref.shape[2]
    half = heads // 2
    me = lax.axis_index("sa")
    ka = lax.axis_index("ka")
    vert = lax.axis_index("vert")
    pair = me // 2
    x = me % 2
    buddy = me + 1 - 2 * x
    first = pair == 0
    last = pair == pairs - 1

    barrier = pltpu.get_barrier_semaphore()

    def greet(where):
        pl.semaphore_signal(barrier, inc=1, device_id=where, device_id_type=MESH)

    greet({"sa": buddy})
    greet({"ka": 1 - ka})
    greet({"vert": 1 - vert})
    if pairs > 1:

        @pl.when(jnp.logical_not(first))
        def _():
            greet({"sa": me - 2})

        @pl.when(jnp.logical_not(last))
        def _():
            greet({"sa": me + 2})

    def remote(source, target, send, recv, where):
        return pltpu.make_async_remote_copy(
            src_ref=source,
            dst_ref=target,
            send_sem=send,
            recv_sem=recv,
            device_id=where,
            device_id_type=MESH,
        )

    def x_copy(h):
        return remote(own.at[h], peer.at[h], x_send.at[h], x_recv.at[h], {"sa": buddy})

    def d_copy():
        return remote(decay, decay_in, d_send, d_recv, {"sa": buddy})

    def f_copy(h):
        return remote(f_out.at[h], f_in.at[h], f_send.at[h], f_recv.at[h], {"sa": me + 2})

    def b_copy(h):
        return remote(b_out.at[h], b_in.at[h], b_send.at[h], b_recv.at[h], {"sa": me - 2})

    def q_copy(h, slot):
        return remote(qk.at[h], qk_in.at[slot], q_send.at[slot], q_recv.at[slot], {"vert": 1 - vert})

    def v_copy(h, slot):
        return remote(vg.at[h], vg_in.at[slot], v_send.at[slot], v_recv.at[slot], {"ka": 1 - ka})

    def stage(c, carry):
        for source, target in ((q_ref, qs), (k_ref, ks), (v_ref, vs), (g_ref, gs), (o_ref, os)):
            piece = source[pl.ds(c * 8, 8)].astype(F32)
            target[pl.ds(pl.multiple_of(c * 8 * heads, 8 * heads), 8 * heads), :] = piece.reshape(
                8 * heads, source.shape[2]
            )
        return carry

    lax.fori_loop(0, rows // 8, stage, 0)

    def head_of(s):
        return (s % 2) * half + s // 2

    def rows_of(h):
        return pl.ds(h, rows, stride=heads)

    ri = lax.broadcasted_iota(jnp.int32, (rows, rows), 0)
    ci = lax.broadcasted_iota(jnp.int32, (rows, rows), 1)
    lower = ri >= ci
    upper = ri <= ci
    tri = lower.astype(F32).astype(BF16)
    upper_ones = upper.astype(F32).astype(BF16)
    lanes = lax.broadcasted_iota(jnp.int32, (kc, 128), 1)
    token_lanes = lax.broadcasted_iota(jnp.int32, (rows, 128), 1)

    def decays(h, total):
        pick = (token_lanes == h).astype(F32).astype(BF16)
        return total + mm(gs[rows_of(h), :].astype(BF16), pick, TN)

    decay[...] = lax.fori_loop(0, heads, decays, jnp.zeros((kc, 128), F32))

    pl.semaphore_wait(
        barrier, 3 + (jnp.where(first, 0, 1) + jnp.where(last, 0, 1) if pairs > 1 else 0)
    )
    d_copy().start()

    mid = rows // 2 - 1

    def states(s, carry):
        h = head_of(s)
        g = gs[rows_of(h), :].astype(BF16)
        cum = mm(tri, g, NN)
        at_mid = cum[mid : mid + 1, :]
        at_end = cum[rows - 1 : rows, :]
        up = jnp.exp(cum - at_mid)
        down = jnp.exp(at_mid - cum)
        to_mid = jnp.exp(at_mid)
        to_end = jnp.exp(at_end - at_mid)
        grow[h] = up
        shrink[h] = down
        ends[h, 0:8, :] = jnp.broadcast_to(to_mid, (8, kc))
        ends[h, 8:16, :] = jnp.broadcast_to(to_end, (8, kc))
        key_high, key_low = split(ks[rows_of(h), :] * (down * to_end))
        query_high, query_low = split(qs[rows_of(h), :] * (up * to_mid) * factor)
        value = vs[rows_of(h), :].astype(BF16)
        cot = os[rows_of(h), :].astype(BF16)
        own[h, 0] = mm(key_high, value, TN) + mm(key_low, value, TN)
        own[h, 1] = mm(query_high, cot, TN) + mm(query_low, cot, TN)
        x_copy(h).start()
        return carry

    lax.fori_loop(0, heads, states, 0)
    d_copy().wait_recv()

    def column(ref, h):
        return jnp.exp(jnp.sum(jnp.where(lanes == h, ref[...], 0.0), axis=1, keepdims=True))

    def local(h):
        value = vs[rows_of(h), :].astype(BF16)
        cot = os[rows_of(h), :].astype(BF16)
        key_high, key_low = split(ks[rows_of(h), :] * shrink[h])
        query_high, query_low = split(qs[rows_of(h), :] * grow[h] * factor)
        s_high, s_low = split(jnp.where(lower, mm(cot, value, NT), 0.0))
        query_local = mm(s_high, key_high, NN) + mm(s_high, key_low, NN) + mm(s_low, key_high, NN)
        t_high, t_low = split(jnp.where(upper, mm(value, cot, NT), 0.0))
        key_local = (
            mm(t_high, query_high, NN) + mm(t_high, query_low, NN) + mm(t_low, query_high, NN)
        )
        qk[h, 0:rows, :] = jnp.concatenate([query_local, key_local], axis=1)
        weights = (
            mm(key_high, query_high, NT) + mm(key_high, query_low, NT) + mm(key_low, query_high, NT)
        )
        w_high, w_low = split(jnp.where(upper, weights, 0.0))
        vg[h] = mm(w_high, cot, NN) + mm(w_low, cot, NN)

    def forward(h):
        state = jnp.where(first, 0.0, f_in[h])
        e_own = column(decay, h)
        e_peer = column(decay_in, h)
        arrived = jnp.where(x == 1, peer[h, 0] + e_peer * state, state)
        entry[h] = arrived
        finish = e_own * arrived + own[h, 0]
        f_out[h] = jnp.where(x == 1, finish, e_peer * finish + peer[h, 0])

    def backward(h):
        state = jnp.where(last, 0.0, b_in[h])
        e_own = column(decay, h)
        e_peer = column(decay_in, h)
        arrived = jnp.where(x == 0, peer[h, 1] + e_peer * state, state)
        leave[h] = arrived
        start = e_own * arrived + own[h, 1]
        b_out[h] = jnp.where(x == 0, start, e_peer * start + peer[h, 1])

    def final(h):
        value = vs[rows_of(h), :].astype(BF16)
        cot = os[rows_of(h), :].astype(BF16)
        before = entry[h]
        after = leave[h]
        to_mid = ends[h, 0:1, :]
        to_end = ends[h, 8:9, :]
        i_high, i_low = split(before)
        o_high, o_low = split(after)
        query_carried = mm(cot, i_high, NT) + mm(cot, i_low, NT)
        key_carried = mm(value, o_high, NT) + mm(value, o_low, NT)
        both = qk[h, 0:rows, :]
        up = grow[h]
        down = shrink[h]
        query_part = up * (both[:, :kc] + to_mid * query_carried) * factor
        key_part = down * (both[:, kc:] + to_end * key_carried)
        qk[h, 0:rows, :] = jnp.concatenate([query_part, key_part], axis=1)
        key_high, key_low = split(ks[rows_of(h), :] * (down * to_end))
        vg[h] = vg[h] + (
            mm(key_high, o_high, NN) + mm(key_high, o_low, NN) + mm(key_low, o_high, NN)
        )
        crossing = (column(decay, h) * before + own[h, 0]) * after
        c_high, c_low = split(crossing)
        ones = jnp.ones((8, vc), BF16)
        beyond = mm(ones, c_high, NT) + mm(ones, c_low, NT)
        qk[h, rows : rows + 8, :] = jnp.concatenate([beyond, beyond], axis=1)

    wait_end = LAG * (pairs - 1)
    f_lag = LAG * pair
    b_lag = LAG * (pairs - 1 - pair)
    c_lag = jnp.maximum(f_lag, b_lag)

    def step(s, carry):
        @pl.when(s < heads)
        def _():
            h = head_of(s)
            local(h)
            x_copy(h).wait_recv()

        fs = s - f_lag

        @pl.when(jnp.logical_and(fs >= 0, fs < heads))
        def _():
            h = head_of(fs)
            if pairs > 1:

                @pl.when(jnp.logical_not(first))
                def _():
                    f_copy(h).wait_recv()

            forward(h)
            if pairs > 1:

                @pl.when(jnp.logical_not(last))
                def _():
                    f_copy(h).start()

        bs = s - b_lag

        @pl.when(jnp.logical_and(bs >= 0, bs < heads))
        def _():
            h = head_of(bs)
            if pairs > 1:

                @pl.when(jnp.logical_not(last))
                def _():
                    b_copy(h).wait_recv()

            backward(h)
            if pairs > 1:

                @pl.when(jnp.logical_not(first))
                def _():
                    b_copy(h).start()

        cs = s - c_lag

        @pl.when(jnp.logical_and(cs >= 0, cs < heads))
        def _():
            h = head_of(cs)
            final(h)
            slot = h % half

            @pl.when(h // half != vert)
            def _():
                q_copy(h, slot).start()

            @pl.when(h // half != ka)
            def _():
                v_copy(h, slot).start()

        return carry

    lax.fori_loop(0, heads + wait_end, step, 0)

    def combine(i, carry):
        h = vert * half + i
        q_copy(h, i).wait_recv()
        total = qk[h] + qk_in[i]
        query_grad = total[0:rows, :kc]
        key_grad = total[0:rows, kc:]
        dq_ref[pl.ds(i, rows, stride=half), :] = query_grad
        dk_ref[pl.ds(i, rows, stride=half), :] = key_grad
        position = qs[rows_of(h), :] * query_grad - ks[rows_of(h), :] * key_grad
        p_high, p_low = split(position)
        sums = mm(upper_ones, p_high, NN) + mm(upper_ones, p_low, NN)
        dg_ref[pl.ds(i, rows, stride=half), :] = sums + total[rows : rows + 1, :kc]
        hv = ka * half + i
        v_copy(hv, i).wait_recv()
        dv_ref[pl.ds(i, rows, stride=half), :] = vg[hv] + vg_in[i]
        return carry

    lax.fori_loop(0, half, combine, 0)

    d_copy().wait_send()

    def drain(h, carry):
        x_copy(h).wait_send()
        if pairs > 1:

            @pl.when(jnp.logical_not(last))
            def _():
                f_copy(h).wait_send()

            @pl.when(jnp.logical_not(first))
            def _():
                b_copy(h).wait_send()

        return carry

    lax.fori_loop(0, heads, drain, 0)

    def drain_parts(i, carry):
        q_copy((1 - vert) * half + i, i).wait_send()
        v_copy((1 - ka) * half + i, i).wait_send()
        return carry

    lax.fori_loop(0, half, drain_parts, 0)


def shards(queries, key_rows, values, log_decays, output_grad):
    rows, heads, kc = queries.shape
    vc = values.shape[2]
    n = lax.axis_size("sa")
    half = heads // 2
    factor = (kc * lax.axis_size("ka")) ** -0.5
    dma = pltpu.SemaphoreType.DMA
    vmem = pl.BlockSpec(memory_space=pltpu.VMEM)
    narrow = jax.ShapeDtypeStruct((rows * half, kc), F32)
    wide = jax.ShapeDtypeStruct((rows * half, vc), F32)
    outs = pl.pallas_call(
        functools.partial(kernel, n, n // 2, factor),
        out_shape=(narrow, narrow, wide, narrow),
        in_specs=[vmem] * 5,
        out_specs=(vmem,) * 4,
        scratch_shapes=[
            pltpu.VMEM((rows * heads, kc), F32),
            pltpu.VMEM((rows * heads, kc), F32),
            pltpu.VMEM((rows * heads, vc), F32),
            pltpu.VMEM((rows * heads, kc), F32),
            pltpu.VMEM((rows * heads, vc), F32),
            pltpu.VMEM((heads, rows, kc), F32),
            pltpu.VMEM((heads, rows, kc), F32),
            pltpu.VMEM((heads, 16, kc), F32),
            pltpu.VMEM((kc, 128), F32),
            pltpu.VMEM((kc, 128), F32),
            pltpu.VMEM((heads, 2, kc, vc), F32),
            pltpu.VMEM((heads, 2, kc, vc), F32),
            pltpu.VMEM((heads, kc, vc), F32),
            pltpu.VMEM((heads, kc, vc), F32),
            pltpu.VMEM((heads, kc, vc), F32),
            pltpu.VMEM((heads, kc, vc), F32),
            pltpu.VMEM((heads, kc, vc), F32),
            pltpu.VMEM((heads, kc, vc), F32),
            pltpu.VMEM((heads, rows + 8, 2 * kc), F32),
            pltpu.VMEM((half, rows + 8, 2 * kc), F32),
            pltpu.VMEM((heads, rows, vc), F32),
            pltpu.VMEM((half, rows, vc), F32),
            dma((heads,)),
            dma((heads,)),
            dma((heads,)),
            dma((heads,)),
            dma((heads,)),
            dma((heads,)),
            dma((half,)),
            dma((half,)),
            dma((half,)),
            dma((half,)),
            dma,
            dma,
        ],
        compiler_params=pltpu.CompilerParams(
            collective_id=0, has_side_effects=True, vmem_limit_bytes=48 * 1024 * 1024
        ),
    )(queries, key_rows, values, log_decays, output_grad)
    query_grad, key_grad, value_grad, decay_grad = outs
    return (
        query_grad.reshape(rows, half, kc),
        key_grad.reshape(rows, half, kc),
        value_grad.reshape(rows, half, vc),
        decay_grad.reshape(rows, half, kc),
    )


def solution(mesh):
    return jax.shard_map(
        shards,
        mesh=mesh,
        in_specs=(
            P("sa", None, "ka"),
            P("sa", None, "ka"),
            P("sa", None, "vert"),
            P("sa", None, "ka"),
            P("sa", None, "vert"),
        ),
        out_specs=(
            P("sa", "vert", "ka"),
            P("sa", "vert", "ka"),
            P("sa", "ka", "vert"),
            P("sa", "vert", "ka"),
        ),
        check_vma=False,
    )
```

time: 259 us -> 61.9 us (0.24)
  waiting for transfers between devices: 71.2 us -> 0 us
  blocking collectives: 63.7 us -> 0 us
  Pallas kernels: 0 us -> 50.4 us
  other arithmetic: 45.7 us -> 0 us
  matrix products: 26.8 us -> 0 us
  local copies, waits for them, and re-layouts: 35 us -> 10.5 us
  between operations: 14.1 us -> 0.72 us
    all_gather x2 -> x0, waiting for transfers between devices: 71 us -> none  [entering(): pieces = jax.tree.map(lambda part: lax.all_gather(part, axis), value)]
    all_gather x2 -> x0, blocking collectives: 63.7 us -> none  [the longest x1 33.1 us: entering(): pieces = jax.tree.map(lambda part: lax.all_gather(part, axis), value)]
    pallas_call x0 -> x1, Pallas kernels: none -> 50.4 us  [shards(): pl.pallas_call(functools.partial(kernel, n, n // 2, factor), out_shape=(n...]
    dot_general x12 -> x0, matrix products: 26.8 us -> none  [the longest x1 4.09 us: gradient_core(): jnp.einsum('nhij,nhjk->nhik', scores, shrunk_key, precision=largest_entry)]
    select_n x14 -> x0, other arithmetic: 19.4 us -> none  [hop(): jnp.where(position < mine, new, old)]
    another operation x3 -> x0, other arithmetic: 14.6 us -> none  [the longest x1 13.2 us: gradient_core(): cumulative = jnp.cumsum(to_blocks(log_decays, TILE_LEN), axis=2)]
    mul x21 -> x0, local copies, waits for them, and re-layouts: 10.3 us -> none  [the longest x14 4.96 us: compose(): return (earlier[0] * later[0], later[0][..., None] * earlier[1] + later[1])]
    unnamed x22 -> x25, local copies, waits for them, and re-layouts: 1.65 us -> 10.5 us
  transfers between devices with their start and end apart: 5 -> 0, of which waited for: 2 -> 0; matrix products, arithmetic and copies ran while one was open for 31% -> 0% of each run, Pallas kernels for 0% -> 0%
where the time goes in v1:
time: 61.9 us; the launch traced here: 61.6 us
  Pallas kernels  50.4 us (81%)
  local copies, waits for them, and re-layouts  10.5 us (17%)
  between operations  0.72 us (1%)
    pallas_call x1, Pallas kernels, shards(): pl.pallas_call(functools.partial(kernel, n, n // 2, factor), out_shape=(n...  50.4 us
    unnamed x25, local copies, waits for them, and re-layouts  10.5 us

profile of v1, /device:TPU:0, one launch (start us, length us, event | category | flops | bytes accessed | tf_op | source)
XLA Modules:
  0.0 61.6 jit_solution(1498061345102927056)
XLA Ops:
  0.6 0.0 copy-start.7
  0.6 1.4 %copy.9.q_ref = bf16[128,16,64]{2,1,0:T(8,128)(2,1)S(1)} copy(bf16[128,16,64]{0,2,1:T(8,128)(2,1)} %param.5) | data formatting | bytes 524288 | tf_op args[0]
  2.1 0.0 copy-done.7
  2.1 0.0 copy-start.8
  2.1 0.0 copy-start.1
  2.1 0.4 copy.10.k_ref
  2.5 0.5 copy-done.8
  3.0 0.0 copy-start
  3.0 0.4 copy.11.g_ref
  3.5 0.0 copy-done.1
  3.5 0.6 %copy-done = bf16[128,16,128]{2,1,0:T(8,128)(2,1)S(1)} copy-done((bf16[128,16,128]{2,1,0:T(8,128)(2,1)S(1)}, bf16[128,16,128]{2,1,0:T(8,128)(2,1)}, u32[]{:S(2)}) %copy-start) | copy-done | bytes 524312
  4.1 50.4 %shard_map.84 = (f32[1024,64]{1,0:T(8,128)S(1)}, f32[1024,64]{1,0:T(8,128)S(1)}, f32[1024,128]{1,0:T(8,128)S(1)}, f32[1024,64]{1,0:T(8,128)S(1)}) custom-call(bf16[128,16,64]{2,1,0:T(8,128)(2,1)S(1)} %copy.9.q_ref, bf16[128,16,64]{2,1,0:T(8,128)(2,1)S(1)} %copy.10.k_ref, bf16[128,16,128]{2,1,0:T(8,128)(2,1)S(1)} %copy-done, ...), custom_call_target="tpu_custom_call" | custom-call | tf_op jit(solution)/shard_map/pallas_call | solution.py:388
  54.5 0.0 copy-start.2
  54.5 0.8 %copy-done.2 = f32[1024,64]{1,0:T(8,128)} copy-done((f32[1024,64]{1,0:T(8,128)}, f32[1024,64]{1,0:T(8,128)S(1)}, u32[]{:S(2)}) %copy-start.2) | copy-done | bytes 262168
  55.3 0.0 copy-start.4
  55.3 0.8 %copy-done.4 = f32[1024,64]{1,0:T(8,128)} copy-done((f32[1024,64]{1,0:T(8,128)}, f32[1024,64]{1,0:T(8,128)S(1)}, u32[]{:S(2)}) %copy-start.4) | copy-done | bytes 262168
  56.1 0.0 copy-start.5
  56.1 0.8 %copy-done.5 = f32[1024,128]{1,0:T(8,128)} copy-done((f32[1024,128]{1,0:T(8,128)}, f32[1024,128]{1,0:T(8,128)S(1)}, u32[]{:S(2)}) %copy-start.5) | copy-done | bytes 524312
  56.9 0.0 copy-start.3
  56.9 2.0 %copy.12 = f32[128,8,64]{0,2,1:T(8,128)} copy(f32[128,8,64]{2,1,0:T(8,128)} %bitcast.6) | data formatting | bytes 524288
  58.9 0.0 copy-done.3
  58.9 0.9 %copy.13 = f32[128,8,64]{0,2,1:T(8,128)} copy(f32[128,8,64]{2,1,0:T(8,128)S(1)} %bitcast.5) | data formatting | bytes 524288
  59.8 0.0 copy-start.6
  59.8 0.9 %copy.14 = f32[128,8,64]{0,2,1:T(8,128)} copy(f32[128,8,64]{2,1,0:T(8,128)S(1)} %bitcast.4) | data formatting | bytes 524288
  60.7 0.1 copy-done.6
  60.9 0.8 %copy.16 = f32[128,8,128]{2,1,0:T(8,128)} copy(f32[128,8,128]{2,1,0:T(8,128)S(1)} %bitcast.7) | data formatting | bytes 1048576
Async XLA Ops:
  0.6 1.4 %copy-start.7 = (bf16[128,16,64]{0,2,1:T(8,128)(2,1)S(1)}, bf16[128,16,64]{0,2,1:T(8,128)(2,1)}, u32[]{:S(2)}) copy-start(bf16[128,16,64]{0,2,1:T(8,128)(2,1)} %param.6) | copy-start | bytes 786436
  2.1 1.0 %copy-start.8 = (bf16[128,16,64]{0,2,1:T(8,128)(2,1)S(1)}, bf16[128,16,64]{0,2,1:T(8,128)(2,1)}, u32[]{:S(2)}) copy-start(bf16[128,16,64]{0,2,1:T(8,128)(2,1)} %param.8) | copy-start | bytes 786436
  2.1 1.4 %copy-start.1 = (bf16[128,16,128]{2,1,0:T(8,128)(2,1)S(1)}, bf16[128,16,128]{2,1,0:T(8,128)(2,1)}, u32[]{:S(2)}) copy-start(bf16[128,16,128]{2,1,0:T(8,128)(2,1)} %o_ref.1) | copy-start | bytes 1572868
  3.0 1.1 %copy-start = (bf16[128,16,128]{2,1,0:T(8,128)(2,1)S(1)}, bf16[128,16,128]{2,1,0:T(8,128)(2,1)}, u32[]{:S(2)}) copy-start(bf16[128,16,128]{2,1,0:T(8,128)(2,1)} %v_ref.1) | copy-start | bytes 1572868
  54.5 0.8 %copy-start.2 = (f32[1024,64]{1,0:T(8,128)}, f32[1024,64]{1,0:T(8,128)S(1)}, u32[]{:S(2)}) copy-start(f32[1024,64]{1,0:T(8,128)S(1)} %get-tuple-element.9) | copy-start | bytes 786436
  55.3 0.8 %copy-start.4 = (f32[1024,64]{1,0:T(8,128)}, f32[1024,64]{1,0:T(8,128)S(1)}, u32[]{:S(2)}) copy-start(f32[1024,64]{1,0:T(8,128)S(1)} %get-tuple-element.8) | copy-start | bytes 786436
  56.1 0.8 %copy-start.5 = (f32[1024,128]{1,0:T(8,128)}, f32[1024,128]{1,0:T(8,128)S(1)}, u32[]{:S(2)}) copy-start(f32[1024,128]{1,0:T(8,128)S(1)} %get-tuple-element.10) | copy-start | bytes 1572868
  56.9 2.0 %copy-start.3 = (f32[1024,64]{1,0:T(8,128)S(1)}, f32[1024,64]{1,0:T(8,128)}, u32[]{:S(2)}) copy-start(f32[1024,64]{1,0:T(8,128)} %copy-done.2) | copy-start | bytes 786436
  59.8 1.0 %copy-start.6 = (f32[1024,128]{1,0:T(8,128)S(1)}, f32[1024,128]{1,0:T(8,128)}, u32[]{:S(2)}) copy-start(f32[1024,128]{1,0:T(8,128)} %copy-done.5) | copy-start | bytes 1572868

commit v2 on v1

--- a/solution.py
+++ b/solution.py
@@ -39,10 +39,7 @@
     dk_ref,
     dv_ref,
     dg_ref,
-    qs,
-    ks,
     vs,
-    gs,
     os,
     grow,
     shrink,
@@ -74,7 +71,7 @@
     d_send,
     d_recv,
 ):
-    rows, heads, kc = q_ref.shape
+    heads, kc, rows = q_ref.shape
     vc = v_ref.shape[2]
     half = heads // 2
     me = lax.axis_index("sa")
@@ -133,7 +130,7 @@
         return remote(vg.at[h], vg_in.at[slot], v_send.at[slot], v_recv.at[slot], {"ka": 1 - ka})
 
     def stage(c, carry):
-        for source, target in ((q_ref, qs), (k_ref, ks), (v_ref, vs), (g_ref, gs), (o_ref, os)):
+        for source, target in ((v_ref, vs), (o_ref, os)):
             piece = source[pl.ds(c * 8, 8)].astype(F32)
             target[pl.ds(pl.multiple_of(c * 8 * heads, 8 * heads), 8 * heads), :] = piece.reshape(
                 8 * heads, source.shape[2]
@@ -152,14 +149,13 @@
     ci = lax.broadcasted_iota(jnp.int32, (rows, rows), 1)
     lower = ri >= ci
     upper = ri <= ci
-    tri = lower.astype(F32).astype(BF16)
     upper_ones = upper.astype(F32).astype(BF16)
+    lower_ones = lower.astype(F32).astype(BF16)
     lanes = lax.broadcasted_iota(jnp.int32, (kc, 128), 1)
-    token_lanes = lax.broadcasted_iota(jnp.int32, (rows, 128), 1)
 
     def decays(h, total):
-        pick = (token_lanes == h).astype(F32).astype(BF16)
-        return total + mm(gs[rows_of(h), :].astype(BF16), pick, TN)
+        pick = (ci == h).astype(F32).astype(BF16)
+        return total + mm(g_ref[h], pick, NN)
 
     decay[...] = lax.fori_loop(0, heads, decays, jnp.zeros((kc, 128), F32))
 
@@ -172,24 +168,23 @@
 
     def states(s, carry):
         h = head_of(s)
-        g = gs[rows_of(h), :].astype(BF16)
-        cum = mm(tri, g, NN)
-        at_mid = cum[mid : mid + 1, :]
-        at_end = cum[rows - 1 : rows, :]
+        cum = mm(g_ref[h], upper_ones, NN)
+        at_mid = cum[:, mid : mid + 1]
+        at_end = cum[:, rows - 1 : rows]
         up = jnp.exp(cum - at_mid)
         down = jnp.exp(at_mid - cum)
         to_mid = jnp.exp(at_mid)
         to_end = jnp.exp(at_end - at_mid)
         grow[h] = up
         shrink[h] = down
-        ends[h, 0:8, :] = jnp.broadcast_to(to_mid, (8, kc))
-        ends[h, 8:16, :] = jnp.broadcast_to(to_end, (8, kc))
-        key_high, key_low = split(ks[rows_of(h), :] * (down * to_end))
-        query_high, query_low = split(qs[rows_of(h), :] * (up * to_mid) * factor)
+        ends[h, 0] = jnp.broadcast_to(to_mid, (kc, rows))
+        ends[h, 1] = jnp.broadcast_to(to_end, (kc, rows))
+        key_high, key_low = split(k_ref[h].astype(F32) * (down * to_end))
+        query_high, query_low = split(q_ref[h].astype(F32) * (up * to_mid) * factor)
         value = vs[rows_of(h), :].astype(BF16)
         cot = os[rows_of(h), :].astype(BF16)
-        own[h, 0] = mm(key_high, value, TN) + mm(key_low, value, TN)
-        own[h, 1] = mm(query_high, cot, TN) + mm(query_low, cot, TN)
+        own[h, 0] = mm(key_high, value, NN) + mm(key_low, value, NN)
+        own[h, 1] = mm(query_high, cot, NN) + mm(query_low, cot, NN)
         x_copy(h).start()
         return carry
 
@@ -202,17 +197,16 @@
     def local(h):
         value = vs[rows_of(h), :].astype(BF16)
         cot = os[rows_of(h), :].astype(BF16)
-        key_high, key_low = split(ks[rows_of(h), :] * shrink[h])
-        query_high, query_low = split(qs[rows_of(h), :] * grow[h] * factor)
+        key_high, key_low = split(k_ref[h].astype(F32) * shrink[h])
+        query_high, query_low = split(q_ref[h].astype(F32) * grow[h] * factor)
+        t_high, t_low = split(jnp.where(upper, mm(value, cot, NT), 0.0))
+        qk[h, 0:kc] = mm(key_high, t_high, NN) + mm(key_low, t_high, NN) + mm(key_high, t_low, NN)
         s_high, s_low = split(jnp.where(lower, mm(cot, value, NT), 0.0))
-        query_local = mm(s_high, key_high, NN) + mm(s_high, key_low, NN) + mm(s_low, key_high, NN)
-        t_high, t_low = split(jnp.where(upper, mm(value, cot, NT), 0.0))
-        key_local = (
-            mm(t_high, query_high, NN) + mm(t_high, query_low, NN) + mm(t_low, query_high, NN)
+        qk[h, kc : 2 * kc] = (
+            mm(query_high, s_high, NN) + mm(query_low, s_high, NN) + mm(query_high, s_low, NN)
         )
-        qk[h, 0:rows, :] = jnp.concatenate([query_local, key_local], axis=1)
         weights = (
-            mm(key_high, query_high, NT) + mm(key_high, query_low, NT) + mm(key_low, query_high, NT)
+            mm(key_high, query_high, TN) + mm(key_high, query_low, TN) + mm(key_low, query_high, TN)
         )
         w_high, w_low = split(jnp.where(upper, weights, 0.0))
         vg[h] = mm(w_high, cot, NN) + mm(w_low, cot, NN)
@@ -240,27 +234,22 @@
         cot = os[rows_of(h), :].astype(BF16)
         before = entry[h]
         after = leave[h]
-        to_mid = ends[h, 0:1, :]
-        to_end = ends[h, 8:9, :]
+        to_mid = ends[h, 0]
+        to_end = ends[h, 1]
         i_high, i_low = split(before)
         o_high, o_low = split(after)
-        query_carried = mm(cot, i_high, NT) + mm(cot, i_low, NT)
-        key_carried = mm(value, o_high, NT) + mm(value, o_low, NT)
-        both = qk[h, 0:rows, :]
-        up = grow[h]
+        query_carried = mm(i_high, cot, NT) + mm(i_low, cot, NT)
+        key_carried = mm(o_high, value, NT) + mm(o_low, value, NT)
         down = shrink[h]
-        query_part = up * (both[:, :kc] + to_mid * query_carried) * factor
-        key_part = down * (both[:, kc:] + to_end * key_carried)
-        qk[h, 0:rows, :] = jnp.concatenate([query_part, key_part], axis=1)
-        key_high, key_low = split(ks[rows_of(h), :] * (down * to_end))
+        qk[h, 0:kc] = grow[h] * (qk[h, 0:kc] + to_mid * query_carried) * factor
+        qk[h, kc : 2 * kc] = down * (qk[h, kc : 2 * kc] + to_end * key_carried)
+        key_high, key_low = split(k_ref[h].astype(F32) * (down * to_end))
         vg[h] = vg[h] + (
-            mm(key_high, o_high, NN) + mm(key_high, o_low, NN) + mm(key_low, o_high, NN)
+            mm(key_high, o_high, TN) + mm(key_high, o_low, TN) + mm(key_low, o_high, TN)
         )
         crossing = (column(decay, h) * before + own[h, 0]) * after
-        c_high, c_low = split(crossing)
-        ones = jnp.ones((8, vc), BF16)
-        beyond = mm(ones, c_high, NT) + mm(ones, c_low, NT)
-        qk[h, rows : rows + 8, :] = jnp.concatenate([beyond, beyond], axis=1)
+        beyond = jnp.sum(crossing, axis=1, keepdims=True)
+        qk[h, 2 * kc : 3 * kc] = jnp.broadcast_to(beyond, (kc, rows))
 
     wait_end = LAG * (pairs - 1)
     f_lag = LAG * pair
@@ -333,15 +322,14 @@
     def combine(i, carry):
         h = vert * half + i
         q_copy(h, i).wait_recv()
-        total = qk[h] + qk_in[i]
-        query_grad = total[0:rows, :kc]
-        key_grad = total[0:rows, kc:]
-        dq_ref[pl.ds(i, rows, stride=half), :] = query_grad
-        dk_ref[pl.ds(i, rows, stride=half), :] = key_grad
-        position = qs[rows_of(h), :] * query_grad - ks[rows_of(h), :] * key_grad
+        query_grad = qk[h, 0:kc] + qk_in[i, 0:kc]
+        key_grad = qk[h, kc : 2 * kc] + qk_in[i, kc : 2 * kc]
+        dq_ref[i] = query_grad
+        dk_ref[i] = key_grad
+        position = q_ref[h].astype(F32) * query_grad - k_ref[h].astype(F32) * key_grad
         p_high, p_low = split(position)
-        sums = mm(upper_ones, p_high, NN) + mm(upper_ones, p_low, NN)
-        dg_ref[pl.ds(i, rows, stride=half), :] = sums + total[rows : rows + 1, :kc]
+        sums = mm(p_high, lower_ones, NN) + mm(p_low, lower_ones, NN)
+        dg_ref[i] = sums + (qk[h, 2 * kc : 3 * kc] + qk_in[i, 2 * kc : 3 * kc])
         hv = ka * half + i
         v_copy(hv, i).wait_recv()
         dv_ref[pl.ds(i, rows, stride=half), :] = vg[hv] + vg_in[i]
@@ -383,7 +371,7 @@
     factor = (kc * lax.axis_size("ka")) ** -0.5
     dma = pltpu.SemaphoreType.DMA
     vmem = pl.BlockSpec(memory_space=pltpu.VMEM)
-    narrow = jax.ShapeDtypeStruct((rows * half, kc), F32)
+    narrow = jax.ShapeDtypeStruct((half, kc, rows), F32)
     wide = jax.ShapeDtypeStruct((rows * half, vc), F32)
     outs = pl.pallas_call(
         functools.partial(kernel, n, n // 2, factor),
@@ -391,14 +379,11 @@
         in_specs=[vmem] * 5,
         out_specs=(vmem,) * 4,
         scratch_shapes=[
-            pltpu.VMEM((rows * heads, kc), F32),
-            pltpu.VMEM((rows * heads, kc), F32),
             pltpu.VMEM((rows * heads, vc), F32),
-            pltpu.VMEM((rows * heads, kc), F32),
             pltpu.VMEM((rows * heads, vc), F32),
-            pltpu.VMEM((heads, rows, kc), F32),
-            pltpu.VMEM((heads, rows, kc), F32),
-            pltpu.VMEM((heads, 16, kc), F32),
+            pltpu.VMEM((heads, kc, rows), F32),
+            pltpu.VMEM((heads, kc, rows), F32),
+            pltpu.VMEM((heads, 2, kc, rows), F32),
             pltpu.VMEM((kc, 128), F32),
             pltpu.VMEM((kc, 128), F32),
             pltpu.VMEM((heads, 2, kc, vc), F32),
@@ -409,8 +394,8 @@
             pltpu.VMEM((heads, kc, vc), F32),
             pltpu.VMEM((heads, kc, vc), F32),
             pltpu.VMEM((heads, kc, vc), F32),
-            pltpu.VMEM((heads, rows + 8, 2 * kc), F32),
-            pltpu.VMEM((half, rows + 8, 2 * kc), F32),
+            pltpu.VMEM((heads, 3 * kc, rows), F32),
+            pltpu.VMEM((half, 3 * kc, rows), F32),
             pltpu.VMEM((heads, rows, vc), F32),
             pltpu.VMEM((half, rows, vc), F32),
             dma((heads,)),
@@ -429,13 +414,19 @@
         compiler_params=pltpu.CompilerParams(
             collective_id=0, has_side_effects=True, vmem_limit_bytes=48 * 1024 * 1024
         ),
-    )(queries, key_rows, values, log_decays, output_grad)
+    )(
+        queries.transpose(1, 2, 0),
+        key_rows.transpose(1, 2, 0),
+        values,
+        log_decays.transpose(1, 2, 0),
+        output_grad,
+    )
     query_grad, key_grad, value_grad, decay_grad = outs
     return (
-        query_grad.reshape(rows, half, kc),
-        key_grad.reshape(rows, half, kc),
+        query_grad.transpose(2, 0, 1),
+        key_grad.transpose(2, 0, 1),
         value_grad.reshape(rows, half, vc),
-        decay_grad.reshape(rows, half, kc),
+        decay_grad.transpose(2, 0, 1),
     )
 
 

time: 61.9 us -> 57.7 us (0.932)
  local copies, waits for them, and re-layouts: 10.5 us -> 7.83 us
  Pallas kernels: 50.4 us -> 48.9 us
    unnamed x25 -> x14, local copies, waits for them, and re-layouts: 10.5 us -> 7.83 us
    pallas_call x1, Pallas kernels: 50.4 us -> 48.9 us  [shards(): pl.pallas_call(functools.partial(kernel, n, n // 2, factor), out_shape=(n...]
where the time goes in v2:
time: 57.7 us; the launch traced here: 57.4 us
  Pallas kernels  48.9 us (85%)
  local copies, waits for them, and re-layouts  7.83 us (14%)
  between operations  0.65 us (1%)
    pallas_call x1, Pallas kernels, shards(): pl.pallas_call(functools.partial(kernel, n, n // 2, factor), out_shape=(n...  48.9 us
    unnamed x14, local copies, waits for them, and re-layouts  7.83 us

profile of v2, /device:TPU:0, one launch (start us, length us, event | category | flops | bytes accessed | tf_op | source)
XLA Modules:
  0.0 57.4 jit_solution(1335781808068117947)
XLA Ops:
  0.6 0.0 copy-start
  0.6 1.0 %copy-done = bf16[128,16,128]{2,1,0:T(8,128)(2,1)S(1)} copy-done((bf16[128,16,128]{2,1,0:T(8,128)(2,1)S(1)}, bf16[128,16,128]{2,1,0:T(8,128)(2,1)}, u32[]{:S(2)}) %copy-start) | copy-done | bytes 524312
  1.7 0.0 copy-start.1
  1.7 1.0 %copy-done.1 = bf16[128,16,128]{2,1,0:T(8,128)(2,1)S(1)} copy-done((bf16[128,16,128]{2,1,0:T(8,128)(2,1)S(1)}, bf16[128,16,128]{2,1,0:T(8,128)(2,1)}, u32[]{:S(2)}) %copy-start.1) | copy-done | bytes 524312
  2.7 0.0 copy-start.2
  2.7 0.9 %copy-done.2 = bf16[128,16,64]{0,2,1:T(8,128)(2,1)S(1)} copy-done((bf16[128,16,64]{0,2,1:T(8,128)(2,1)S(1)}, bf16[128,16,64]{0,2,1:T(8,128)(2,1)}, u32[]{:S(2)}) %copy-start.2) | copy-done | bytes 262168
  3.7 0.0 copy-start.3
  3.7 0.9 %copy-done.3 = bf16[128,16,64]{0,2,1:T(8,128)(2,1)S(1)} copy-done((bf16[128,16,64]{0,2,1:T(8,128)(2,1)S(1)}, bf16[128,16,64]{0,2,1:T(8,128)(2,1)}, u32[]{:S(2)}) %copy-start.3) | copy-done | bytes 262168
  4.6 0.0 copy-start.4
  4.6 0.9 %copy-done.4 = bf16[128,16,64]{0,2,1:T(8,128)(2,1)S(1)} copy-done((bf16[128,16,64]{0,2,1:T(8,128)(2,1)S(1)}, bf16[128,16,64]{0,2,1:T(8,128)(2,1)}, u32[]{:S(2)}) %copy-start.4) | copy-done | bytes 262168
  5.6 48.9 %shard_map.84 = (f32[8,64,128]{2,1,0:T(8,128)S(1)}, f32[8,64,128]{2,1,0:T(8,128)S(1)}, f32[1024,128]{1,0:T(8,128)S(1)}, f32[8,64,128]{2,1,0:T(8,128)S(1)}) custom-call(bf16[16,64,128]{2,1,0:T(8,128)(2,1)S(1)} %bitcast.8, bf16[16,64,128]{2,1,0:T(8,128)(2,1)S(1)} %bitcast.9, bf16[128,16,128]{2,1,0:T(8,128)(2,1)S(1)} %copy-done, ...), custom_call_target="tpu_custom_call" | custom-call | tf_op jit(solution)/shard_map/pallas_call | solution.py:376
  54.5 0.7 %copy.13 = f32[128,8,64]{0,2,1:T(8,128)} copy(f32[128,8,64]{0,2,1:T(8,128)S(1)} %bitcast.13) | data formatting | bytes 524288
  55.2 0.7 %copy.14 = f32[128,8,64]{0,2,1:T(8,128)} copy(f32[128,8,64]{0,2,1:T(8,128)S(1)} %bitcast.12) | data formatting | bytes 524288
  55.9 0.8 %copy.15 = f32[128,8,128]{2,1,0:T(8,128)} copy(f32[128,8,128]{2,1,0:T(8,128)S(1)} %bitcast.7) | data formatting | bytes 1048576
  56.7 0.7 %copy.16 = f32[128,8,64]{0,2,1:T(8,128)} copy(f32[128,8,64]{0,2,1:T(8,128)S(1)} %bitcast.11) | data formatting | bytes 524288
Async XLA Ops:
  0.6 1.0 %copy-start = (bf16[128,16,128]{2,1,0:T(8,128)(2,1)S(1)}, bf16[128,16,128]{2,1,0:T(8,128)(2,1)}, u32[]{:S(2)}) copy-start(bf16[128,16,128]{2,1,0:T(8,128)(2,1)} %v_ref.1) | copy-start | bytes 1572868
  1.7 1.0 %copy-start.1 = (bf16[128,16,128]{2,1,0:T(8,128)(2,1)S(1)}, bf16[128,16,128]{2,1,0:T(8,128)(2,1)}, u32[]{:S(2)}) copy-start(bf16[128,16,128]{2,1,0:T(8,128)(2,1)} %o_ref.1) | copy-start | bytes 1572868
  2.7 0.9 %copy-start.2 = (bf16[128,16,64]{0,2,1:T(8,128)(2,1)S(1)}, bf16[128,16,64]{0,2,1:T(8,128)(2,1)}, u32[]{:S(2)}) copy-start(bf16[128,16,64]{0,2,1:T(8,128)(2,1)} %param.5) | copy-start | bytes 786436
  3.7 0.9 %copy-start.3 = (bf16[128,16,64]{0,2,1:T(8,128)(2,1)S(1)}, bf16[128,16,64]{0,2,1:T(8,128)(2,1)}, u32[]{:S(2)}) copy-start(bf16[128,16,64]{0,2,1:T(8,128)(2,1)} %param.6) | copy-start | bytes 786436
  4.6 0.9 %copy-start.4 = (bf16[128,16,64]{0,2,1:T(8,128)(2,1)S(1)}, bf16[128,16,64]{0,2,1:T(8,128)(2,1)}, u32[]{:S(2)}) copy-start(bf16[128,16,64]{0,2,1:T(8,128)(2,1)} %param.8) | copy-start | bytes 786436

commit v3 on v2

--- a/solution.py
+++ b/solution.py
@@ -30,17 +30,26 @@
     n,
     pairs,
     factor,
+    q_hbm,
+    k_hbm,
+    v_hbm,
+    g_hbm,
+    o_hbm,
+    dq_ref,
+    dk_ref,
+    dv_ref,
+    dg_ref,
     q_ref,
     k_ref,
     v_ref,
     g_ref,
     o_ref,
-    dq_ref,
-    dk_ref,
-    dv_ref,
-    dg_ref,
     vs,
     os,
+    vb,
+    ob,
+    e_own,
+    e_peer,
     grow,
     shrink,
     ends,
@@ -52,6 +61,7 @@
     b_in,
     f_out,
     b_out,
+    x_out,
     entry,
     leave,
     qk,
@@ -70,10 +80,24 @@
     v_recv,
     d_send,
     d_recv,
+    y_send,
+    y_recv,
+    w_send,
+    w_recv,
+    in_sem,
 ):
     heads, kc, rows = q_ref.shape
     vc = v_ref.shape[2]
     half = heads // 2
+    quarter = half // 2
+    loads = [
+        pltpu.make_async_copy(source, target, in_sem.at[i])
+        for i, (source, target) in enumerate(
+            ((g_hbm, g_ref), (v_hbm, v_ref), (o_hbm, o_ref), (k_hbm, k_ref), (q_hbm, q_ref))
+        )
+    ]
+    for load in loads:
+        load.start()
     me = lax.axis_index("sa")
     ka = lax.axis_index("ka")
     vert = lax.axis_index("vert")
@@ -114,6 +138,16 @@
     def x_copy(h):
         return remote(own.at[h], peer.at[h], x_send.at[h], x_recv.at[h], {"sa": buddy})
 
+    def y_copy(h):
+        return remote(
+            x_out.at[h, 0], peer.at[h, 0], y_send.at[h], y_recv.at[h], {"sa": buddy}
+        )
+
+    def w_copy(h):
+        return remote(
+            x_out.at[h, 1], peer.at[h, 1], w_send.at[h], w_recv.at[h], {"sa": buddy}
+        )
+
     def d_copy():
         return remote(decay, decay_in, d_send, d_recv, {"sa": buddy})
 
@@ -129,18 +163,11 @@
     def v_copy(h, slot):
         return remote(vg.at[h], vg_in.at[slot], v_send.at[slot], v_recv.at[slot], {"ka": 1 - ka})
 
-    def stage(c, carry):
-        for source, target in ((v_ref, vs), (o_ref, os)):
-            piece = source[pl.ds(c * 8, 8)].astype(F32)
-            target[pl.ds(pl.multiple_of(c * 8 * heads, 8 * heads), 8 * heads), :] = piece.reshape(
-                8 * heads, source.shape[2]
-            )
-        return carry
-
-    lax.fori_loop(0, rows // 8, stage, 0)
-
-    def head_of(s):
-        return (s % 2) * half + s // 2
+    def first_set(j):
+        return (j % 2) * half + j // 2
+
+    def second_set(j):
+        return first_set(j) + quarter
 
     def rows_of(h):
         return pl.ds(h, rows, stride=heads)
@@ -153,21 +180,36 @@
     lower_ones = lower.astype(F32).astype(BF16)
     lanes = lax.broadcasted_iota(jnp.int32, (kc, 128), 1)
 
-    def decays(h, total):
-        pick = (ci == h).astype(F32).astype(BF16)
-        return total + mm(g_ref[h], pick, NN)
-
-    decay[...] = lax.fori_loop(0, heads, decays, jnp.zeros((kc, 128), F32))
+    loads[0].wait()
+    ones = jnp.ones((rows, 128), BF16)
+    packed = jnp.zeros((kc, 128), F32)
+    for h in range(heads):
+        total = mm(g_ref[h], ones, NN)
+        e_own[h] = jnp.exp(total)
+        packed = jnp.where(lanes == h, total, packed)
+    decay[...] = packed
 
     pl.semaphore_wait(
         barrier, 3 + (jnp.where(first, 0, 1) + jnp.where(last, 0, 1) if pairs > 1 else 0)
     )
     d_copy().start()
 
+    for load in loads[1:]:
+        load.wait()
+
+    def stage(c, carry):
+        for source, target in ((v_ref, vs), (o_ref, os)):
+            piece = source[pl.ds(c * 8, 8)].astype(F32)
+            target[pl.ds(pl.multiple_of(c * 8 * heads, 8 * heads), 8 * heads), :] = piece.reshape(
+                8 * heads, source.shape[2]
+            )
+        return carry
+
+    lax.fori_loop(0, rows // 8, stage, 0, unroll=4)
+
     mid = rows // 2 - 1
 
-    def states(s, carry):
-        h = head_of(s)
+    def states(h):
         cum = mm(g_ref[h], upper_ones, NN)
         at_mid = cum[:, mid : mid + 1]
         at_end = cum[:, rows - 1 : rows]
@@ -183,20 +225,27 @@
         query_high, query_low = split(q_ref[h].astype(F32) * (up * to_mid) * factor)
         value = vs[rows_of(h), :].astype(BF16)
         cot = os[rows_of(h), :].astype(BF16)
+        vb[h] = value
+        ob[h] = cot
         own[h, 0] = mm(key_high, value, NN) + mm(key_low, value, NN)
         own[h, 1] = mm(query_high, cot, NN) + mm(query_low, cot, NN)
-        x_copy(h).start()
-        return carry
-
-    lax.fori_loop(0, heads, states, 0)
+
+    def early(i, carry):
+        for j in (2 * i, 2 * i + 1):
+            states(first_set(j))
+        for j in (2 * i, 2 * i + 1):
+            x_copy(first_set(j)).start()
+        return carry
+
+    lax.fori_loop(0, quarter, early, 0)
     d_copy().wait_recv()
-
-    def column(ref, h):
-        return jnp.exp(jnp.sum(jnp.where(lanes == h, ref[...], 0.0), axis=1, keepdims=True))
+    received = decay_in[...]
+    for h in range(heads):
+        e_peer[h] = jnp.exp(jnp.broadcast_to(received[:, h : h + 1], (kc, 128)))
 
     def local(h):
-        value = vs[rows_of(h), :].astype(BF16)
-        cot = os[rows_of(h), :].astype(BF16)
+        value = vb[h]
+        cot = ob[h]
         key_high, key_low = split(k_ref[h].astype(F32) * shrink[h])
         query_high, query_low = split(q_ref[h].astype(F32) * grow[h] * factor)
         t_high, t_low = split(jnp.where(upper, mm(value, cot, NT), 0.0))
@@ -211,29 +260,39 @@
         w_high, w_low = split(jnp.where(upper, weights, 0.0))
         vg[h] = mm(w_high, cot, NN) + mm(w_low, cot, NN)
 
-    def forward(h):
+    def forward_pair(h):
         state = jnp.where(first, 0.0, f_in[h])
-        e_own = column(decay, h)
-        e_peer = column(decay_in, h)
-        arrived = jnp.where(x == 1, peer[h, 0] + e_peer * state, state)
+        arrived = jnp.where(x == 1, peer[h, 0] + e_peer[h] * state, state)
         entry[h] = arrived
-        finish = e_own * arrived + own[h, 0]
-        f_out[h] = jnp.where(x == 1, finish, e_peer * finish + peer[h, 0])
-
-    def backward(h):
+        finish = e_own[h] * arrived + own[h, 0]
+        f_out[h] = jnp.where(x == 1, finish, e_peer[h] * finish + peer[h, 0])
+
+    def backward_pair(h):
         state = jnp.where(last, 0.0, b_in[h])
-        e_own = column(decay, h)
-        e_peer = column(decay_in, h)
-        arrived = jnp.where(x == 0, peer[h, 1] + e_peer * state, state)
+        arrived = jnp.where(x == 0, peer[h, 1] + e_peer[h] * state, state)
         leave[h] = arrived
-        start = e_own * arrived + own[h, 1]
-        b_out[h] = jnp.where(x == 0, start, e_peer * start + peer[h, 1])
-
-    def final(h):
-        value = vs[rows_of(h), :].astype(BF16)
-        cot = os[rows_of(h), :].astype(BF16)
-        before = entry[h]
-        after = leave[h]
+        start = e_own[h] * arrived + own[h, 1]
+        b_out[h] = jnp.where(x == 0, start, e_peer[h] * start + peer[h, 1])
+
+    def forward_column(h):
+        state = jnp.where(first, 0.0, f_in[h])
+        finish = e_own[h] * state + own[h, 0]
+        across = e_peer[h] * state
+        entry[h] = jnp.where(x == 0, state, across)
+        x_out[h, 0] = jnp.where(x == 0, finish, state)
+        f_out[h] = jnp.where(x == 0, e_peer[h] * finish, e_own[h] * across + own[h, 0])
+
+    def backward_column(h):
+        state = jnp.where(last, 0.0, b_in[h])
+        start = e_own[h] * state + own[h, 1]
+        across = e_peer[h] * state
+        leave[h] = jnp.where(x == 1, state, across)
+        x_out[h, 1] = jnp.where(x == 1, start, state)
+        b_out[h] = jnp.where(x == 1, e_peer[h] * start, e_own[h] * across + own[h, 1])
+
+    def final(h, before, after):
+        value = vb[h]
+        cot = ob[h]
         to_mid = ends[h, 0]
         to_end = ends[h, 1]
         i_high, i_low = split(before)
@@ -247,77 +306,117 @@
         vg[h] = vg[h] + (
             mm(key_high, o_high, TN) + mm(key_high, o_low, TN) + mm(key_low, o_high, TN)
         )
-        crossing = (column(decay, h) * before + own[h, 0]) * after
+        crossing = (e_own[h] * before + own[h, 0]) * after
         beyond = jnp.sum(crossing, axis=1, keepdims=True)
         qk[h, 2 * kc : 3 * kc] = jnp.broadcast_to(beyond, (kc, rows))
 
-    wait_end = LAG * (pairs - 1)
     f_lag = LAG * pair
     b_lag = LAG * (pairs - 1 - pair)
     c_lag = jnp.maximum(f_lag, b_lag)
-
-    def step(s, carry):
-        @pl.when(s < heads)
-        def _():
-            h = head_of(s)
-            local(h)
-            x_copy(h).wait_recv()
-
-        fs = s - f_lag
-
-        @pl.when(jnp.logical_and(fs >= 0, fs < heads))
-        def _():
-            h = head_of(fs)
-            if pairs > 1:
-
-                @pl.when(jnp.logical_not(first))
-                def _():
-                    f_copy(h).wait_recv()
-
-            forward(h)
-            if pairs > 1:
-
-                @pl.when(jnp.logical_not(last))
-                def _():
-                    f_copy(h).start()
-
-        bs = s - b_lag
-
-        @pl.when(jnp.logical_and(bs >= 0, bs < heads))
-        def _():
-            h = head_of(bs)
-            if pairs > 1:
-
-                @pl.when(jnp.logical_not(last))
-                def _():
-                    b_copy(h).wait_recv()
-
-            backward(h)
-            if pairs > 1:
-
-                @pl.when(jnp.logical_not(first))
-                def _():
-                    b_copy(h).start()
-
-        cs = s - c_lag
-
-        @pl.when(jnp.logical_and(cs >= 0, cs < heads))
-        def _():
-            h = head_of(cs)
-            final(h)
-            slot = h % half
-
-            @pl.when(h // half != vert)
+    second_lag = max(half, LAG * (pairs - 1) + 2)
+
+    def forward_in(h):
+        if pairs > 1:
+
+            @pl.when(jnp.logical_not(first))
             def _():
-                q_copy(h, slot).start()
-
-            @pl.when(h // half != ka)
+                f_copy(h).wait_recv()
+
+    def forward_on(h):
+        if pairs > 1:
+
+            @pl.when(jnp.logical_not(last))
             def _():
-                v_copy(h, slot).start()
-
-        return carry
-
-    lax.fori_loop(0, heads + wait_end, step, 0)
+                f_copy(h).start()
+
+    def backward_in(h):
+        if pairs > 1:
+
+            @pl.when(jnp.logical_not(last))
+            def _():
+                b_copy(h).wait_recv()
+
+    def backward_on(h):
+        if pairs > 1:
+
+            @pl.when(jnp.logical_not(first))
+            def _():
+                b_copy(h).start()
+
+    def send_parts(h):
+        slot = h % half
+
+        @pl.when(h // half != vert)
+        def _():
+            q_copy(h, slot).start()
+
+        @pl.when(h // half != ka)
+        def _():
+            v_copy(h, slot).start()
+
+    def inside(j):
+        return jnp.logical_and(j >= 0, j < half)
+
+    def step(t, carry):
+        @pl.when(t < half)
+        def _():
+            states(second_set(t))
+            local(first_set(t))
+            x_copy(first_set(t)).wait_recv()
+
+        @pl.when(inside(t - half))
+        def _():
+            local(second_set(t - half))
+
+        fj = t - f_lag
+
+        @pl.when(inside(fj))
+        def _():
+            column = second_set(fj)
+            forward_in(column)
+            forward_column(column)
+            forward_on(column)
+            y_copy(column).start()
+            paired = first_set(fj)
+            forward_in(paired)
+            forward_pair(paired)
+            forward_on(paired)
+
+        bj = t - b_lag
+
+        @pl.when(inside(bj))
+        def _():
+            column = second_set(bj)
+            backward_in(column)
+            backward_column(column)
+            backward_on(column)
+            w_copy(column).start()
+            paired = first_set(bj)
+            backward_in(paired)
+            backward_pair(paired)
+            backward_on(paired)
+
+        cj = t - c_lag
+
+        @pl.when(inside(cj))
+        def _():
+            h = first_set(cj)
+            final(h, entry[h], leave[h])
+            send_parts(h)
+
+        sj = t - second_lag
+
+        @pl.when(inside(sj))
+        def _():
+            h = second_set(sj)
+            y_copy(h).wait_recv()
+            w_copy(h).wait_recv()
+            final(h, entry[h] + peer[h, 0], leave[h] + peer[h, 1])
+            send_parts(h)
+
+        return carry
+
+    lax.fori_loop(0, half + second_lag, step, 0)
 
     def combine(i, carry):
         h = vert * half + i
@@ -340,7 +439,6 @@
     d_copy().wait_send()
 
     def drain(h, carry):
-        x_copy(h).wait_send()
         if pairs > 1:
 
             @pl.when(jnp.logical_not(last))
@@ -354,6 +452,14 @@
         return carry
 
     lax.fori_loop(0, heads, drain, 0)
+
+    def drain_x(j, carry):
+        x_copy(first_set(j)).wait_send()
+        y_copy(second_set(j)).wait_send()
+        w_copy(second_set(j)).wait_send()
+        return carry
+
+    lax.fori_loop(0, half, drain_x, 0)
 
     def drain_parts(i, carry):
         q_copy((1 - vert) * half + i, i).wait_send()
@@ -376,11 +482,20 @@
     outs = pl.pallas_call(
         functools.partial(kernel, n, n // 2, factor),
         out_shape=(narrow, narrow, wide, narrow),
-        in_specs=[vmem] * 5,
+        in_specs=[pl.BlockSpec(memory_space=pltpu.HBM)] * 5,
         out_specs=(vmem,) * 4,
         scratch_shapes=[
+            pltpu.VMEM((heads, kc, rows), BF16),
+            pltpu.VMEM((heads, kc, rows), BF16),
+            pltpu.VMEM((rows, heads, vc), BF16),
+            pltpu.VMEM((heads, kc, rows), BF16),
+            pltpu.VMEM((rows, heads, vc), BF16),
             pltpu.VMEM((rows * heads, vc), F32),
             pltpu.VMEM((rows * heads, vc), F32),
+            pltpu.VMEM((heads, rows, vc), BF16),
+            pltpu.VMEM((heads, rows, vc), BF16),
+            pltpu.VMEM((heads, kc, 128), F32),
+            pltpu.VMEM((heads, kc, 128), F32),
             pltpu.VMEM((heads, kc, rows), F32),
             pltpu.VMEM((heads, kc, rows), F32),
             pltpu.VMEM((heads, 2, kc, rows), F32),
@@ -392,6 +507,7 @@
             pltpu.VMEM((heads, kc, vc), F32),
             pltpu.VMEM((heads, kc, vc), F32),
             pltpu.VMEM((heads, kc, vc), F32),
+            pltpu.VMEM((heads, 2, kc, vc), F32),
             pltpu.VMEM((heads, kc, vc), F32),
             pltpu.VMEM((heads, kc, vc), F32),
             pltpu.VMEM((heads, 3 * kc, rows), F32),
@@ -410,9 +526,14 @@
             dma((half,)),
             dma,
             dma,
+            dma((heads,)),
+            dma((heads,)),
+            dma((heads,)),
+            dma((heads,)),
+            dma((5,)),
         ],
         compiler_params=pltpu.CompilerParams(
-            collective_id=0, has_side_effects=True, vmem_limit_bytes=48 * 1024 * 1024
+            collective_id=0, has_side_effects=True, vmem_limit_bytes=67043328
         ),
     )(
         queries.transpose(1, 2, 0),

time: 57.7 us -> 44 us (0.76)
  Pallas kernels: 48.9 us -> 38.9 us
  local copies, waits for them, and re-layouts: 7.83 us -> 4.25 us
    pallas_call x1, Pallas kernels: 48.9 us -> 38.9 us  [shards(): pl.pallas_call(functools.partial(kernel, n, n // 2, factor), out_shape=(n...]
    unnamed x14 -> x10, local copies, waits for them, and re-layouts: 7.83 us -> 4.25 us
where the time goes in v3:
time: 44 us; the launch traced here: 43.8 us
  Pallas kernels  38.9 us (88%)
  local copies, waits for them, and re-layouts  4.25 us (10%)
  between operations  0.66 us (2%)
    pallas_call x1, Pallas kernels, shards(): pl.pallas_call(functools.partial(kernel, n, n // 2, factor), out_shape=(n...  38.9 us
    unnamed x10, local copies, waits for them, and re-layouts  4.25 us

profile of v3, /device:TPU:0, one launch (start us, length us, event | category | flops | bytes accessed | tf_op | source)
XLA Modules:
  0.0 43.8 jit_solution(17956817487666573950)
XLA Ops:
  0.6 38.9 %shard_map.84 = (f32[8,64,128]{2,1,0:T(8,128)}, f32[8,64,128]{2,1,0:T(8,128)}, f32[1024,128]{1,0:T(8,128)}, f32[8,64,128]{2,1,0:T(8,128)}) custom-call(bf16[16,64,128]{2,1,0:T(8,128)(2,1)} %bitcast.8, bf16[16,64,128]{2,1,0:T(8,128)(2,1)} %bitcast.9, bf16[128,16,128]{2,1,0:T(8,128)(2,1)} %v_hbm.1, bf16[16,64,128]{2,1,0:T(8,128)(2,1)} %bitcast.10, ...), custom_call_target="tpu_custom_call" | custom-call | tf_op jit(solution)/shard_map/pallas_call | solution.py:482
  39.5 0.0 copy-start.2
  39.5 0.0 copy-start
  39.5 1.7 %copy.13 = f32[128,8,64]{0,2,1:T(8,128)} copy(f32[128,8,64]{0,2,1:T(8,128)} %bitcast.13) | data formatting | bytes 524288
  41.3 0.0 copy-done.2
  41.3 0.7 %copy.14 = f32[128,8,64]{0,2,1:T(8,128)} copy(f32[128,8,64]{0,2,1:T(8,128)S(1)} %bitcast.12) | data formatting | bytes 524288
  42.0 0.0 copy-done
  42.0 0.0 copy-start.1
  42.0 0.8 %copy.15 = f32[128,8,128]{2,1,0:T(8,128)} copy(f32[128,8,128]{2,1,0:T(8,128)S(1)} %bitcast.7) | data formatting | bytes 1048576
  42.8 0.3 copy-done.1
  43.1 0.7 %copy.16 = f32[128,8,64]{0,2,1:T(8,128)} copy(f32[128,8,64]{0,2,1:T(8,128)S(1)} %bitcast.11) | data formatting | bytes 524288
Async XLA Ops:
  39.5 1.8 %copy-start.2 = (f32[8,64,128]{2,1,0:T(8,128)S(1)}, f32[8,64,128]{2,1,0:T(8,128)}, u32[]{:S(2)}) copy-start(f32[8,64,128]{2,1,0:T(8,128)} %get-tuple-element.9) | copy-start | bytes 786436
  39.5 2.5 %copy-start = (f32[1024,128]{1,0:T(8,128)S(1)}, f32[1024,128]{1,0:T(8,128)}, u32[]{:S(2)}) copy-start(f32[1024,128]{1,0:T(8,128)} %get-tuple-element.10) | copy-start | bytes 1572868
  42.0 1.1 %copy-start.1 = (f32[8,64,128]{2,1,0:T(8,128)S(1)}, f32[8,64,128]{2,1,0:T(8,128)}, u32[]{:S(2)}) copy-start(f32[8,64,128]{2,1,0:T(8,128)} %get-tuple-element.11) | copy-start | bytes 786436

commit v4 on v3

--- a/solution.py
+++ b/solution.py
@@ -469,6 +469,16 @@
     lax.fori_loop(0, half, drain_parts, 0)
 
 
+def place(*refs):
+    copies = [
+        pltpu.make_async_copy(refs[i], refs[4 + i], refs[8].at[i]) for i in (2, 0, 1, 3)
+    ]
+    for copy in copies:
+        copy.start()
+    for copy in copies:
+        copy.wait()
+
+
 def shards(queries, key_rows, values, log_decays, output_grad):
     rows, heads, kc = queries.shape
     vc = values.shape[2]
@@ -481,7 +491,7 @@
     wide = jax.ShapeDtypeStruct((rows * half, vc), F32)
     outs = pl.pallas_call(
         functools.partial(kernel, n, n // 2, factor),
-        out_shape=(narrow, narrow, wide, narrow),
+        out_shape=tuple(pltpu.VMEM(a.shape, a.dtype) for a in (narrow, narrow, wide, narrow)),
         in_specs=[pl.BlockSpec(memory_space=pltpu.HBM)] * 5,
         out_specs=(vmem,) * 4,
         scratch_shapes=[
@@ -533,7 +543,7 @@
             dma((5,)),
         ],
         compiler_params=pltpu.CompilerParams(
-            collective_id=0, has_side_effects=True, vmem_limit_bytes=67043328
+            collective_id=0, has_side_effects=True, vmem_limit_bytes=65200128
         ),
     )(
         queries.transpose(1, 2, 0),
@@ -542,7 +552,14 @@
         log_decays.transpose(1, 2, 0),
         output_grad,
     )
-    query_grad, key_grad, value_grad, decay_grad = outs
+    query_grad, key_grad, value_grad, decay_grad = pl.pallas_call(
+        place,
+        out_shape=(narrow, narrow, wide, narrow),
+        in_specs=[vmem] * 4,
+        out_specs=(pl.BlockSpec(memory_space=pltpu.HBM),) * 4,
+        scratch_shapes=[dma((4,))],
+        compiler_params=pltpu.CompilerParams(vmem_limit_bytes=8 * 1024 * 1024),
+    )(*outs)
     return (
         query_grad.transpose(2, 0, 1),
         key_grad.transpose(2, 0, 1),

time: 44 us -> 39.7 us (0.902)
  local copies, waits for them, and re-layouts: 4.25 us -> 0 us
    unnamed x10 -> x0, local copies, waits for them, and re-layouts: 4.25 us -> none
    pallas_call x1 -> x2, Pallas kernels: 38.9 us -> 38.9 us  [the longest x1 37.8 us: shards(): pl.pallas_call(functools.partial(kernel, n, n // 2, factor), out_shape=tu...]
where the time goes in v4:
time: 39.7 us; the launch traced here: 39.5 us
  Pallas kernels  38.9 us (98%)
  between operations  0.64 us (2%)
    pallas_call x1, Pallas kernels, shards(): pl.pallas_call(functools.partial(kernel, n, n // 2, factor), out_shape=tu...  37.8 us
    pallas_call x1, Pallas kernels, shards(): pl.pallas_call(place, out_shape=(narrow, narrow, wide, narrow), in_specs=...  1.08 us

profile of v4, /device:TPU:0, one launch (start us, length us, event | category | flops | bytes accessed | tf_op | source)
XLA Modules:
  0.0 39.5 jit_solution(14137400137587696164)
XLA Ops:
  0.6 37.8 %shard_map.84 = (f32[8,64,128]{2,1,0:T(8,128)S(1)}, f32[8,64,128]{2,1,0:T(8,128)S(1)}, f32[1024,128]{1,0:T(8,128)S(1)}, f32[8,64,128]{2,1,0:T(8,128)S(1)}) custom-call(bf16[16,64,128]{2,1,0:T(8,128)(2,1)} %bitcast.7, bf16[16,64,128]{2,1,0:T(8,128)(2,1)} %bitcast.8, bf16[128,16,128]{2,1,0:T(8,128)(2,1)} %v_hbm.1, bf16[16,64,128]{2,1,0:T(8,128)(2,1)} %bitcast.9, ...), custom_call_target="tpu_custom_call" | custom-call | tf_op jit(solution)/shard_map/pallas_call | solution.py:492
  38.5 1.1 %shard_map.85 = (f32[8,64,128]{2,1,0:T(8,128)}, f32[8,64,128]{2,1,0:T(8,128)}, f32[1024,128]{1,0:T(8,128)}, f32[8,64,128]{2,1,0:T(8,128)}) custom-call(f32[8,64,128]{2,1,0:T(8,128)S(1)} %get-tuple-element.12.refs_0_, f32[8,64,128]{2,1,0:T(8,128)S(1)} %get-tuple-element.13.refs_1_, f32[1024,128]{1,0:T(8,128)S(1)} %get-tuple-element.14.refs_2_, ...), custom_call_target="tpu_custom_call" | custom-call | tf_op jit(solution)/shard_map/pallas_call | solution.py:555

commit v5 on v4

--- a/solution.py
+++ b/solution.py
@@ -189,11 +189,6 @@
         packed = jnp.where(lanes == h, total, packed)
     decay[...] = packed
 
-    pl.semaphore_wait(
-        barrier, 3 + (jnp.where(first, 0, 1) + jnp.where(last, 0, 1) if pairs > 1 else 0)
-    )
-    d_copy().start()
-
     for load in loads[1:]:
         load.wait()
 
@@ -206,6 +201,11 @@
         return carry
 
     lax.fori_loop(0, rows // 8, stage, 0, unroll=4)
+
+    pl.semaphore_wait(
+        barrier, 3 + (jnp.where(first, 0, 1) + jnp.where(last, 0, 1) if pairs > 1 else 0)
+    )
+    d_copy().start()
 
     mid = rows // 2 - 1
 

time: 39.7 us -> 40 us (level)
  no operation moved by 1% of the time
where the time goes in v5:
time: 40 us; the launch traced here: 39.8 us
  Pallas kernels  39.2 us (98%)
  between operations  0.64 us (2%)
    pallas_call x1, Pallas kernels, shards(): pl.pallas_call(functools.partial(kernel, n, n // 2, factor), out_shape=tu...  38.1 us
    pallas_call x1, Pallas kernels, shards(): pl.pallas_call(place, out_shape=(narrow, narrow, wide, narrow), in_specs=...  1.08 us

profile of v5, /device:TPU:0, one launch (start us, length us, event | category | flops | bytes accessed | tf_op | source)
XLA Modules:
  0.0 39.8 jit_solution(5076618112215731200)
XLA Ops:
  0.6 38.1 %shard_map.84 = (f32[8,64,128]{2,1,0:T(8,128)S(1)}, f32[8,64,128]{2,1,0:T(8,128)S(1)}, f32[1024,128]{1,0:T(8,128)S(1)}, f32[8,64,128]{2,1,0:T(8,128)S(1)}) custom-call(bf16[16,64,128]{2,1,0:T(8,128)(2,1)} %bitcast.7, bf16[16,64,128]{2,1,0:T(8,128)(2,1)} %bitcast.8, bf16[128,16,128]{2,1,0:T(8,128)(2,1)} %v_hbm.1, bf16[16,64,128]{2,1,0:T(8,128)(2,1)} %bitcast.9, ...), custom_call_target="tpu_custom_call" | custom-call | tf_op jit(solution)/shard_map/pallas_call | solution.py:492
  38.8 1.1 %shard_map.85 = (f32[8,64,128]{2,1,0:T(8,128)}, f32[8,64,128]{2,1,0:T(8,128)}, f32[1024,128]{1,0:T(8,128)}, f32[8,64,128]{2,1,0:T(8,128)}) custom-call(f32[8,64,128]{2,1,0:T(8,128)S(1)} %get-tuple-element.12.refs_0_, f32[8,64,128]{2,1,0:T(8,128)S(1)} %get-tuple-element.13.refs_1_, f32[1024,128]{1,0:T(8,128)S(1)} %get-tuple-element.14.refs_2_, ...), custom_call_target="tpu_custom_call" | custom-call | tf_op jit(solution)/shard_map/pallas_call | solution.py:555
